TPU v7x, 8 devices: a whole 2x2x1 slice. The times are simulated.
8 devices in a mesh: batch: 1 (over z), z: 2 (over y), y: 2 (over x), x: 2 (over core).
Axes of the slice: x: 2, y: 2, z: 1, core: 2. Of those that a mesh axis runs over, the one named last changes fastest.
Arguments:
- source: float32 [256, 256, 256], P(('batch', 'z'), 'y', 'x')
- initial_guess: float32 [256, 256, 256], P(('batch', 'z'), 'y', 'x')
Outputs:
- output: float32 [256, 256, 256], P(('batch', 'z'), 'y', 'x')
All inputs are finite; a program needn't handle non-finite values.
Results may differ from a plain program's by a relative error of at most 0.001.
Values sent between devices are 32-bit elements.
A program may use at most 1 GiB of HBM per device.

v0:
```python
import jax
import jax.numpy as jnp
from jax import lax
from jax.sharding import PartitionSpec as P

CYCLES = 2
PRE = 2
POST = 2
COARSE_SWEEPS = 24
GRID_AXES = ('z', 'y', 'x')


def level_count(fine_edge):
    count = 0
    edge_now = fine_edge
    for step_index in range(16):
        if edge_now % 2 == 0 and edge_now // 2 >= 4:
            edge_now = edge_now // 2
            count = count + 1
    return count


def split_level(fine_edge, levels, counts):
    deepest = 0
    for level in range(1, levels + 1):
        if deepest == level - 1 and all((fine_edge >> level) % count == 0 for count in counts):
            deepest = level
    return deepest


def halo_planes(grid, axis, count):
    extent = grid.shape[axis]
    first = lax.slice_in_dim(grid, 0, 1, axis=axis)
    last = lax.slice_in_dim(grid, extent - 1, extent, axis=axis)
    if count == 1:
        return -first, -last
    axis_name = GRID_AXES[axis]
    position = lax.axis_index(axis_name)
    upward = [(rank_id, rank_id + 1) for rank_id in range(count - 1)]
    downward = [(rank_id + 1, rank_id) for rank_id in range(count - 1)]
    from_below = lax.ppermute(last, axis_name, upward)
    from_above = lax.ppermute(first, axis_name, downward)
    lower = jnp.where(position == 0, -first, from_below)
    upper = jnp.where(position == count - 1, -last, from_above)
    return lower, upper


def shifted(grid, axis, count):
    lower, upper = halo_planes(grid, axis, count)
    extent = grid.shape[axis]
    below = jnp.concatenate([lower, lax.slice_in_dim(grid, 0, extent - 1, axis=axis)], axis=axis)
    above = jnp.concatenate([lax.slice_in_dim(grid, 1, extent, axis=axis), upper], axis=axis)
    return below, above


def neighbour_sum(grid, grid_counts):
    total = jnp.zeros_like(grid)
    for axis in range(3):
        below, above = shifted(grid, axis, grid_counts[axis])
        total = total + below + above
    return total


def red_mask(local_shape, grid_counts):
    parity = 0
    for axis in range(3):
        coords = jnp.arange(local_shape[axis], dtype=jnp.int32)
        if grid_counts[axis] > 1:
            coords = coords + lax.axis_index(GRID_AXES[axis]) * local_shape[axis]
        bcast_shape = [1, 1, 1]
        bcast_shape[axis] = local_shape[axis]
        parity = parity + coords.reshape(bcast_shape)
    return parity % 2 == 0


def gs_sweep(iterate, source, step_sq, red_cells, grid_counts):
    scaled = step_sq * source
    updated = (scaled + neighbour_sum(iterate, grid_counts)) / 6.0
    iterate = jnp.where(red_cells, updated, iterate)
    updated = (scaled + neighbour_sum(iterate, grid_counts)) / 6.0
    return jnp.where(red_cells, iterate, updated)


def residual(iterate, source, step_sq, grid_counts):
    return source - (6.0 * iterate - neighbour_sum(iterate, grid_counts)) / step_sq


def restrict(grid):
    grid_shape = grid.shape
    folded = grid.reshape(grid_shape[0] // 2, 2, grid_shape[1] // 2, 2, grid_shape[2] // 2, 2)
    return folded.mean(axis=(1, 3, 5))


def prolong(coarse, grid_counts):
    fine = coarse
    for axis in range(3):
        below, above = shifted(fine, axis, grid_counts[axis])
        even_cells = 0.75 * fine + 0.25 * below
        odd_cells = 0.75 * fine + 0.25 * above
        new_shape = list(fine.shape)
        new_shape[axis] = 2 * new_shape[axis]
        fine = jnp.stack([even_cells, odd_cells], axis=axis + 1).reshape(new_shape)
    return fine


def gather_grid(block, grid_counts):
    whole = block
    for axis in range(3):
        if grid_counts[axis] > 1:
            whole = lax.all_gather(whole, GRID_AXES[axis], axis=axis, tiled=True)
    return whole


def own_block(whole, local_shape, grid_counts):
    starts = []
    for axis in range(3):
        if grid_counts[axis] > 1:
            starts.append(lax.axis_index(GRID_AXES[axis]) * local_shape[axis])
        else:
            starts.append(0)
    return lax.dynamic_slice(whole, starts, local_shape)


def vcycle(iterate, source, level, fine_edge, levels, deepest, grid_counts):
    step_sq = (1.0 / (fine_edge >> level)) ** 2
    red_cells = red_mask(iterate.shape, grid_counts)
    if level == levels:
        return lax.fori_loop(0, COARSE_SWEEPS, lambda sweep_index, current: gs_sweep(current, source, step_sq, red_cells, grid_counts), iterate)
    for sweep_index in range(PRE):
        iterate = gs_sweep(iterate, source, step_sq, red_cells, grid_counts)
    residue = residual(iterate, source, step_sq, grid_counts)
    if level < deepest:
        coarse_source = restrict(residue)
        coarse_sol = vcycle(jnp.zeros_like(coarse_source), coarse_source, level + 1, fine_edge, levels, deepest, grid_counts)
        correction = prolong(coarse_sol, grid_counts)
    else:
        single = (1, 1, 1)
        coarse_source = restrict(gather_grid(residue, grid_counts))
        coarse_sol = vcycle(jnp.zeros_like(coarse_source), coarse_source, level + 1, fine_edge, levels, levels, single)
        correction = own_block(prolong(coarse_sol, single), residue.shape, grid_counts)
    iterate = iterate + correction
    for sweep_index in range(POST):
        iterate = gs_sweep(iterate, source, step_sq, red_cells, grid_counts)
    return iterate


def solution(mesh):
    counts = tuple(mesh.shape[axis_name] for axis_name in GRID_AXES)
    grid_spec = P(('batch', 'z'), 'y', 'x')

    def local_solve(source, initial_guess):
        fine_edge = source.shape[0] * counts[0]
        levels = level_count(fine_edge)
        deepest = split_level(fine_edge, levels, counts)
        iterate = initial_guess
        for cycle_index in range(CYCLES):
            iterate = vcycle(iterate, source, 0, fine_edge, levels, deepest, counts)
        return iterate

    return jax.shard_map(local_solve, mesh=mesh, in_specs=(grid_spec, grid_spec), out_specs=grid_spec, check_vma=False)
```

profile of v0, /device:TPU:0, one launch (start us, length us, event | category | flops | bytes accessed | tf_op | source)
XLA Modules:
  0.0 8152.4 jit_solution(6160369956498536711)
XLA Ops:
  230.9 27.8 fusion.36
  287.8 16.8 copy.1488
  359.2 27.8 fusion.43
  476.8 27.8 fusion.50
  594.2 27.8 fusion.57
  693.1 16.3 negate_select_fusion.43
  711.8 31.0 fusion.64
  752.1 538.6 %reshape.2414 = f32[64,2,64,2,64,2]{5,4,3,2,1,0:T(8,128)} reshape(f32[128,128,128]{2,1,0:T(8,128)} %copy.1505) | data formatting | bytes 16777216 | tf_op jit(solution)/shard_map/reshape | solution.py:90
  1290.8 160.9 %reduce_sum.108 = f32[64,64,64]{2,1,0:T(8,128)} reduce(f32[64,2,64,2,64,2]{5,4,3,2,1,0:T(8,128)} %reshape.2414, f32[]{:T(128)} %constant.395.clone.1), dimensions={1,3,5}, to_apply=%region_0.1 | reduce | flops 1835008 | bytes 9437188 | tf_op jit(solution)/shard_map/reduce_sum | solution.py:91
  1633.3 71.5 reshape.2415
  1704.8 20.8 reduce_sum.109
  2017.9 915.9 %while.22 = (s32[]{:T(128)}, f32[2,2,2]{2,1,0:T(2,128)S(1)}, f32[2,2,2]{2,1,0:T(2,128)S(1)}, s32[2]{0:T(128)S(1)}, s32[2,2]{1,0:T(2,128)S(1)}, /*index=5*/s32[]{:T(128)}, s32[]{:T(128)}, u32[]{:T(128)}, u32[]{:T(128)}) while((s32[]{:T(128)}, f32[2,2,2]{2,1,0:T(2,128)S(1)}, f32[2,2,2]{2,1,0:T(2,128)S(1)}, s32[2]{0:T(128)S(1)}, ...), condition=%wide.region_7.8_spmd.clone, body=%wide.region_6.7_spmd.clone.sunk | while | flops 577 | bytes 3150 | solution.py:128
  3767.8 27.8 fusion.71
  3885.7 27.8 fusion.78
  4003.1 27.8 fusion.85
  4120.7 27.8 fusion.92
  4238.1 27.8 fusion.99
  4355.7 27.8 fusion.106
  4473.1 27.8 fusion.113
  4590.7 27.8 fusion.120
  4689.3 16.3 negate_select_fusion.25
  4708.0 31.0 fusion.127
  4748.4 538.6 %reshape.2438 = f32[64,2,64,2,64,2]{5,4,3,2,1,0:T(8,128)} reshape(f32[128,128,128]{2,1,0:T(8,128)} %copy.1671) | data formatting | bytes 16777216 | tf_op jit(solution)/shard_map/reshape | solution.py:90
  5287.0 160.9 %reduce_sum.114 = f32[64,64,64]{2,1,0:T(8,128)} reduce(f32[64,2,64,2,64,2]{5,4,3,2,1,0:T(8,128)} %reshape.2438, f32[]{:T(128)} %constant.395.clone.1), dimensions={1,3,5}, to_apply=%region_8.9 | reduce | flops 1835008 | bytes 9437188 | tf_op jit(solution)/shard_map/reduce_sum | solution.py:91
  5629.5 71.5 reshape.2439
  5701.0 20.8 reduce_sum.115
  6011.7 912.6 %while.23 = (s32[]{:T(128)}, f32[2,2,2]{2,1,0:T(2,128)S(1)}, f32[2,2,2]{2,1,0:T(2,128)S(1)}, s32[2]{0:T(128)S(1)}, s32[2,2]{1,0:T(2,128)S(1)}, /*index=5*/s32[]{:T(128)}, s32[]{:T(128)}, u32[]{:T(128)}, u32[]{:T(128)}) while((s32[]{:T(128)}, f32[2,2,2]{2,1,0:T(2,128)S(1)}, f32[2,2,2]{2,1,0:T(2,128)S(1)}, s32[2]{0:T(128)S(1)}, ...), condition=%wide.region_15.16_spmd.clone, body=%wide.region_14.15_spmd.clone.sunk | while | flops 577 | bytes 3150 | solution.py:128
  7740.1 16.3 negate_select_fusion.23
  7758.7 27.8 fusion.134
  7876.6 27.8 fusion.141
  7993.9 27.8 fusion.148
  8111.4 31.4 fusion.155
  (5219 shorter events, 5968.0 us)
Async XLA Ops:
  0.0 173.3 %collective-permute-start.59 = (f32[64,64,1]{1,0,2:T(8,128)S(1)}, f32[64,64,1]{1,0,2:T(8,128)S(1)}, u32[]{:S(2)}, u32[]{:S(2)}) collective-permute-start(f32[64,64,1]{1,0,2:T(8,128)S(1)} %broadcast.1446), channel_id=1, source_target_pairs={{1,0},{3,2},{5,4},{7,6}} | collective-permute-start | bytes 49160 | tf_op jit(solution)/shard_map/ppermute | solution.py:42
  1.3 181.8 %collective-permute-start.58 = (f32[64,64,1]{1,0,2:T(8,128)S(1)}, f32[64,64,1]{1,0,2:T(8,128)S(1)}, u32[]{:S(2)}, u32[]{:S(2)}) collective-permute-start(f32[64,64,1]{1,0,2:T(8,128)S(1)} %broadcast.1446), channel_id=1, source_target_pairs={{0,1},{2,3},{4,5},{6,7}} | collective-permute-start | bytes 49160 | tf_op jit(solution)/shard_map/ppermute | solution.py:41
  4.3 87.3 %collective-permute-start.179 = (f32[4,4,1]{2,1,0:T(4,128)S(1)}, f32[4,4,1]{2,1,0:T(4,128)S(1)}, u32[]{:S(2)}, u32[]{:S(2)}) collective-permute-start(f32[4,4,1]{2,1,0:T(4,128)S(1)} %broadcast.1494), channel_id=1, source_target_pairs={{1,0},{3,2},{5,4},{7,6}} | collective-permute-start | bytes 200 | tf_op jit(solution)/shard_map/ppermute | solution.py:42
  5.6 91.9 %collective-permute-start.178 = (f32[4,4,1]{2,1,0:T(4,128)S(1)}, f32[4,4,1]{2,1,0:T(4,128)S(1)}, u32[]{:S(2)}, u32[]{:S(2)}) collective-permute-start(f32[4,4,1]{2,1,0:T(4,128)S(1)} %broadcast.1494), channel_id=1, source_target_pairs={{0,1},{2,3},{4,5},{6,7}} | collective-permute-start | bytes 200 | tf_op jit(solution)/shard_map/ppermute | solution.py:41
  315.6 41.4 collective-permute-start.34
  318.3 38.6 collective-permute-start.35
  433.7 40.8 collective-permute-start.40
  436.2 38.3 collective-permute-start.41
  551.1 40.8 collective-permute-start.46
  553.6 38.3 collective-permute-start.47
  668.6 40.8 collective-permute-start.52
  671.1 38.3 collective-permute-start.53
  3842.3 41.1 collective-permute-start.370
  3845.1 38.3 collective-permute-start.371
  3960.0 40.8 collective-permute-start.376
  3962.5 38.3 collective-permute-start.377
  4077.6 40.8 collective-permute-start.382
  4080.1 38.3 collective-permute-start.383
  4195.0 40.8 collective-permute-start.388
  4197.5 38.3 collective-permute-start.389
  4312.6 40.8 collective-permute-start.394
  4315.1 38.3 collective-permute-start.395
  4430.0 40.8 collective-permute-start.400
  4432.4 38.3 collective-permute-start.401
  4547.6 40.8 collective-permute-start.406
  4550.0 38.3 collective-permute-start.407
  4664.9 40.8 collective-permute-start.412
  4667.3 38.3 collective-permute-start.413
  7833.2 41.1 collective-permute-start.700
  7836.0 38.3 collective-permute-start.701
  7950.9 40.8 collective-permute-start.706
  8068.3 40.8 collective-permute-start.712
  (1443 other events, 18604.3 us)
where the time goes:
time: 8200 us; the launch traced here: 8150 us
  local copies, waits for them, and re-layouts  3060 us (37%)
  starting transfers between devices  2960 us (36%)
  other arithmetic  1680 us (20%)
  waiting for transfers between devices  429 us (5%)
    ppermute x633, starting transfers between devices, halo_planes(): from_below = lax.ppermute(last, axis_name, upward)  2140 us
    reshape x12, local copies, waits for them, and re-layouts, restrict(): grid.reshape(grid_shape[0] // 2, 2, grid_shape[1] // 2, 2, grid_shape[2]...  1240 us
    ppermute x633, starting transfers between devices, halo_planes(): from_above = lax.ppermute(first, axis_name, downward)  819 us
    slice x294, local copies, waits for them, and re-layouts, shifted(): lax.slice_in_dim(grid, 1, extent, axis=axis)  515 us
    ppermute x633, waiting for transfers between devices, halo_planes(): from_above = lax.ppermute(first, axis_name, downward)  426 us
    select_n x321, other arithmetic, halo_planes(): upper = jnp.where(position == count - 1, -last, from_above)  421 us
    slice x330, local copies, waits for them, and re-layouts, halo_planes(): first = lax.slice_in_dim(grid, 0, 1, axis=axis)  389 us
    reduce_sum x12, other arithmetic, restrict(): return folded.mean(axis=(1, 3, 5))  378 us

commit v1 on v0

v1 whole, which is shorter than its diff:
```python
import functools

import jax
import jax.numpy as jnp
from jax import lax
from jax.experimental import pallas as pl
from jax.experimental.pallas import tpu as pltpu
from jax.sharding import PartitionSpec as P

CYCLES = 2
COARSE_SWEEPS = 24
LANES = 128
TILE = 8
MESH = pl.DeviceIdType.MESH
F32 = jnp.float32
SIXTH = 1.0 / 6.0
RED, BLACK = 0, 1
HIGHEST = lax.Precision.HIGHEST


def mult8(value):
    return value if isinstance(value, int) else pl.multiple_of(value, TILE)


def rows(start, size):
    return pl.ds(mult8(start), size)


class Level:
    def __init__(self, n, dist, width, unroll):
        self.n = n
        self.planes = n // 2
        self.nb = max(n, TILE)
        self.pitch = self.nb + 16
        self.dist = dist
        self.width = min(width, self.nb)
        self.chunks = self.nb // self.width
        self.unroll = min(unroll, self.planes)

    def scratch(self):
        cells = pltpu.VMEM(((self.planes + 2) * self.pitch, LANES), F32)
        packed = pltpu.VMEM((self.planes * self.nb, LANES), F32)
        shapes = dict(v0=cells, v1=cells, g0=packed, g1=packed)
        if self.dist:
            face_x = pltpu.VMEM((self.nb, LANES), F32)
            face_y = pltpu.VMEM((self.planes, LANES), F32)
            for colour in (RED, BLACK):
                shapes[f'fx{colour}'] = face_x
                shapes[f'hx{colour}'] = face_x
                shapes[f'fy{colour}'] = face_y
                shapes[f'hy{colour}'] = face_y
            for axis in ('x', 'z'):
                shapes[f's{axis}'] = pltpu.SemaphoreType.DMA((2 * self.chunks,))
                shapes[f'r{axis}'] = pltpu.SemaphoreType.DMA((2 * self.chunks,))
            shapes['sy'] = pltpu.SemaphoreType.DMA((2,))
            shapes['ry'] = pltpu.SemaphoreType.DMA((2,))
        return shapes

    def bind(self, refs):
        self.v = (refs['v0'], refs['v1'])
        self.g = (refs['g0'], refs['g1'])
        if self.dist:
            self.fx = (refs['fx0'], refs['fx1'])
            self.hx = (refs['hx0'], refs['hx1'])
            self.fy = (refs['fy0'], refs['fy1'])
            self.hy = (refs['hy0'], refs['hy1'])
            self.sems = {key: refs[key] for key in ('sx', 'rx', 'sz', 'rz', 'sy', 'ry')}


def make_levels(edge):
    levels = [Level(edge, True, 32, 4), Level(edge // 2, True, 32, 4)]
    n = edge // 2
    while n >= 4:
        levels.append(Level(n, False, 32, 4))
        n = n // 2
    return levels


def kernel_body(names, edge, *args):
    refs = dict(zip(names, args))
    xi, yi, zi = lax.axis_index('x'), lax.axis_index('y'), lax.axis_index('z')
    levels = make_levels(edge)
    for index, level in enumerate(levels):
        prefix = f'L{index}_'
        level.bind({key[len(prefix):]: ref for key, ref in refs.items() if key.startswith(prefix)})

    def lanes(size):
        return lax.broadcasted_iota(jnp.int32, (size, LANES), 1)

    def even_mask(size):
        return lax.rem(lanes(size) + lax.broadcasted_iota(jnp.int32, (size, LANES), 0), 2) == 0

    def side(level):
        return jnp.where(xi == 0, level.n - 1, 0)

    def copy_x(level, colour, j):
        span = rows(j * level.width, level.width)
        k = colour * level.chunks + j
        return pltpu.make_async_remote_copy(
            src_ref=level.fx[colour].at[span], dst_ref=level.hx[colour].at[span],
            send_sem=level.sems['sx'].at[k], recv_sem=level.sems['rx'].at[k],
            device_id={'x': 1 - xi}, device_id_type=MESH)

    def copy_z(level, colour, j):
        offset = TILE + j * level.width
        src = jnp.where(zi == 0, level.planes, 1) * level.pitch + offset
        dst = jnp.where(zi == 0, 0, level.planes + 1) * level.pitch + offset
        k = colour * level.chunks + j
        return pltpu.make_async_remote_copy(
            src_ref=level.v[colour].at[rows(src, level.width)], dst_ref=level.v[colour].at[rows(dst, level.width)],
            send_sem=level.sems['sz'].at[k], recv_sem=level.sems['rz'].at[k],
            device_id={'z': 1 - zi}, device_id_type=MESH)

    def copy_y(level, colour):
        return pltpu.make_async_remote_copy(
            src_ref=level.fy[colour], dst_ref=level.hy[colour],
            send_sem=level.sems['sy'].at[colour], recv_sem=level.sems['ry'].at[colour],
            device_id={'y': 1 - yi}, device_id_type=MESH)

    def wait_y(level, colour):
        copy_y(level, colour).wait()
        ghost = jnp.where(yi == 0, level.n, -1)
        level.v[colour][pl.ds(level.pitch + TILE + ghost, level.planes, stride=level.pitch), :] = level.hy[colour][...]

    def wait_all(level, colour):
        wait_y(level, colour)

        def step(j, carry):
            copy_x(level, colour, j).wait()
            copy_z(level, colour, j).wait()
            return carry
        lax.fori_loop(0, level.chunks, step, 0)

    def fill_ghosts(level, colour):
        own, other = level.v[colour], level.v[1 - colour]
        pitch, n = level.pitch, level.n

        def fill_row(src, dst):
            if level.planes >= TILE:
                values = own[pl.ds(pitch + TILE + src, level.planes, stride=pitch), :]
                other[pl.ds(pitch + TILE + dst, level.planes, stride=pitch), :] = -values
            else:
                for k in range(level.planes):
                    base = (k + 1) * pitch + TILE
                    other[pl.ds(base + dst, 1), :] = -own[pl.ds(base + src, 1), :]

        def fill_plane(src, dst):
            other[rows(dst * pitch + TILE, level.nb), :] = -own[rows(src * pitch + TILE, level.nb), :]

        if level.dist:
            fill_row(jnp.where(yi == 0, 0, n - 1), jnp.where(yi == 0, -1, n))
            fill_plane(jnp.where(zi == 0, 1, level.planes), jnp.where(zi == 0, 0, level.planes + 1))
        else:
            fill_row(0, -1)
            fill_row(n - 1, n)
            fill_plane(1, 0)
            fill_plane(level.planes, level.planes + 1)

    def half_sweep(level, colour, mode):
        own, other, source = level.v[colour], level.v[1 - colour], level.g[colour]
        width, pitch, n, planes = level.width, level.pitch, level.n, level.planes
        stencil = mode in ('gs', 'res0', 'res1')
        sends = level.dist and mode in ('gs', 'zero', 'copy')
        waits = level.dist and mode in ('gs', 'res0')
        if stencil:
            fill_ghosts(level, colour)
        if waits:
            wait_y(level, 1 - colour)
        lane = lanes(width)
        even = even_mask(width)
        takes_below = even if colour == RED else jnp.logical_not(even)
        first_lane, last_lane = lane == 0, lane == n - 1
        if level.dist:
            q = side(level)
            halo_lane = lane == q

        def chunk(jj, carry):
            j = jnp.where(yi == 1, jj, level.chunks - 1 - jj) if level.dist else jj
            if waits:
                copy_x(level, 1 - colour, j).wait()
                copy_z(level, 1 - colour, j).wait()
            row0 = j * width + TILE
            if stencil and level.dist:
                halo = level.hx[1 - colour][rows(j * width, width), :]

            def planes_step(i, state):
                below, here, face = state
                for u in range(level.unroll):
                    k = i * level.unroll + u
                    base = (k + 1) * pitch + row0
                    if mode != 'zero':
                        old = own[rows(base, width), :]
                    if mode == 'copy':
                        new = old
                    elif mode == 'zero':
                        new = source[rows(k * level.nb + j * width, width), :] * SIXTH
                    else:
                        above = other[rows(base + pitch, width), :]
                        total = other[pl.ds(base - 1, width), :] + other[pl.ds(base + 1, width), :]
                        edge_values = -old
                        if level.dist:
                            shift = lax.rem(q - k + LANES, LANES)
                            edge_values = jnp.where(halo_lane, pltpu.roll(halo, shift, 1), edge_values)
                        left = jnp.where(first_lane, edge_values, pltpu.roll(here, 1, 1))
                        right = jnp.where(last_lane, edge_values, pltpu.roll(here, 127, 1))
                        total = total + (left + right) + (here + jnp.where(takes_below, below, above))
                        total = total + source[rows(k * level.nb + j * width, width), :]
                        new = total * SIXTH if mode == 'gs' else total - 6.0 * old
                        below, here = here, above
                    if mode in ('gs', 'zero'):
                        own[rows(base, width), :] = new
                    elif mode == 'res0':
                        refs['stage_u'][rows(k * level.nb + j * width, width), :] = new
                    elif mode == 'res1':
                        span = rows(k * level.nb + j * width, width)
                        refs['stage_u'][span, :] = refs['stage_u'][span, :] + new
                    if sends:
                        face = jnp.where(lane == k, pltpu.roll(new, lax.rem(k - q + LANES, LANES), 1), face)
                return below, here, face

            blank = jnp.zeros((width, LANES), F32)
            if stencil:
                start = (other[rows(row0, width), :], other[rows(pitch + row0, width), :], blank)
            else:
                start = (blank, blank, blank)
            _, _, face = lax.fori_loop(0, planes // level.unroll, planes_step, start)
            if sends:
                level.fx[colour][rows(j * width, width), :] = face
                copy_x(level, colour, j).start()
                copy_z(level, colour, j).start()

                @pl.when(jj == 0)
                def _():
                    y_row = jnp.where(yi == 0, n - 1, 0)
                    level.fy[colour][...] = own[pl.ds(pitch + TILE + y_row, planes, stride=pitch), :]
                    copy_y(level, colour).start()
            return carry

        lax.fori_loop(0, level.chunks, chunk, 0)

    def sweeps(level, count):
        def step(index, carry):
            half_sweep(level, RED, 'gs')
            half_sweep(level, BLACK, 'gs')
            return carry
        lax.fori_loop(0, count, step, 0)

    square_i = lax.broadcasted_iota(jnp.int32, (LANES, LANES), 0)
    square_f = lax.broadcasted_iota(jnp.int32, (LANES, LANES), 1)

    def restriction_matrix(n_coarse):
        hit = (lax.div(square_i, 2) == square_f) & (square_i < 2 * n_coarse)
        return jnp.where(hit, 0.5, 0.0).astype(F32)

    def prolongation_matrix(n_fine, n_coarse, offset, low_lane, high_lane):
        own_index = lax.div(square_f, 2) + offset
        near = jnp.where(lax.rem(square_f, 2) == 0, own_index - 1, own_index + 1)
        outside = (near < 0) | (near > n_coarse - 1)
        value = jnp.where(square_i == own_index, jnp.where(outside & (low_lane is None), 0.5, 0.75), 0.0)
        value = value + jnp.where((square_i == near) & jnp.logical_not(outside), 0.25, 0.0)
        return jnp.where(square_f < n_fine, value, 0.0).astype(F32)

    def distributed_matrix(n_coarse):
        own_index = lax.div(square_f, 2)
        near = jnp.where(lax.rem(square_f, 2) == 0, own_index - 1, own_index + 1)
        halo_near = jnp.where(xi == 0, n_coarse, -1)
        ghost_near = jnp.where(xi == 0, -1, n_coarse)
        lane_of_near = jnp.where(near == -1, 127, near)
        value = jnp.where(square_i == own_index, jnp.where(near == ghost_near, 0.5, 0.75), 0.0)
        inside = (near >= 0) & (near < n_coarse)
        value = value + jnp.where((square_i == lane_of_near) & (inside | (near == halo_near)), 0.25, 0.0)
        return value.astype(F32)

    def matmul(a, b):
        return jnp.dot(a, b, precision=HIGHEST, preferred_element_type=F32)

    stage_u, stage_f = refs['stage_u'], refs['stage_f']

    def restrict_pair(level, k, matrix):
        n_coarse = level.n // 2
        size = max(n_coarse, TILE)
        pair = []
        for z in (0, 1):
            base = (2 * k + z) * level.nb
            total = stage_u[pl.ds(base, size, stride=2), :] + stage_u[pl.ds(base + 1, size, stride=2), :]
            pair.append(matmul(total, matrix))
        even = even_mask(size)
        return jnp.where(even, pair[0], pair[1]), jnp.where(even, pair[1], pair[0])

    def restrict_local(level, coarse, index):
        matrix = refs[f'mat_q{index}'][...]

        def step(k, carry):
            red, black = restrict_pair(level, k, matrix)
            coarse.g[RED][rows(k * coarse.nb, coarse.nb), :] = red
            coarse.g[BLACK][rows(k * coarse.nb, coarse.nb), :] = black
            return carry
        lax.fori_loop(0, coarse.planes, step, 0)

    gather_own, gather_other = refs['gather_own'], refs['gather_other']
    fine_block = levels[1]
    block_n = fine_block.n // 2
    block_rows = (block_n // 4) * block_n
    slot = 2 * zi + yi

    def gather_copies():
        copies = []
        for index, flips in enumerate(((0, 1), (1, 0), (1, 1))):
            target = {'z': zi + flips[0] - 2 * zi * flips[0], 'y': yi + flips[1] - 2 * yi * flips[1]}
            here = gather_own.at[rows(slot * block_rows, block_rows)]
            copies.append(pltpu.make_async_remote_copy(
                src_ref=here, dst_ref=here, send_sem=refs['gs'].at[index], recv_sem=refs['gr'].at[index],
                device_id=target, device_id_type=MESH))
        return copies

    def partner_copy(index):
        flips = ((0, 0), (0, 1), (1, 0), (1, 1))[index]
        z = zi + flips[0] - 2 * zi * flips[0]
        y = yi + flips[1] - 2 * yi * flips[1]
        span = rows((2 * z + y) * block_rows, block_rows)
        return pltpu.make_async_remote_copy(
            src_ref=gather_own.at[span], dst_ref=gather_other.at[span],
            send_sem=refs['ps'].at[index], recv_sem=refs['pr'].at[index],
            device_id={'x': 1 - xi}, device_id_type=MESH)

    def restrict_gather(coarse):
        matrix = refs['mat_q1'][...]

        def step(m, carry):
            packed = None
            for half in (0, 1):
                for colour, part in enumerate(restrict_pair(fine_block, 2 * m + half, matrix)):
                    turn = (2 * half + colour) * block_n
                    part = part if turn == 0 else pltpu.roll(part, turn, 1)
                    packed = part if packed is None else packed + part
            gather_own[rows(slot * block_rows + m * block_n, block_n), :] = packed
            return carry
        lax.fori_loop(0, block_n // 4, step, 0)
        copies = gather_copies()
        for copy in copies:
            copy.start()
        partner_copy(0).start()
        for index, copy in enumerate(copies):
            copy.wait()
            partner_copy(index + 1).start()
        for index in range(4):
            partner_copy(index).wait()
        lane = lanes(block_n)
        low, middle = lane < block_n, lane < 2 * block_n

        for source_slot in range(4):
            zs, ys = source_slot // 2, source_slot % 2

            def unpack(m, carry):
                span = rows(source_slot * block_rows + m * block_n, block_n)
                mine, theirs = gather_own[span, :], gather_other[span, :]
                at_zero = jnp.where(xi == 0, mine, theirs)
                at_one = jnp.where(xi == 0, theirs, mine)
                for group in range(4):
                    half, colour = group // 2, group % 2
                    left = at_zero if group == 0 else pltpu.roll(at_zero, LANES - group * block_n, 1)
                    turn = (LANES - group * block_n + block_n) % LANES
                    right = at_one if turn == 0 else pltpu.roll(at_one, turn, 1)
                    value = jnp.where(low, left, jnp.where(middle, right, 0.0))
                    plane = zs * (block_n // 2) + 2 * m + half
                    coarse.g[colour][rows(plane * coarse.nb + ys * block_n, block_n), :] = value
                return carry
            lax.fori_loop(0, block_n // 4, unpack, 0)

    def set_zero(ref, size):
        def step(i, carry):
            ref[rows(i * TILE, TILE), :] = jnp.zeros((TILE, LANES), F32)
            return carry
        lax.fori_loop(0, size // TILE, step, 0)

    def expand_x(coarse, planes_ref, matrix):
        nb, pitch = coarse.nb, coarse.pitch
        lane = lanes(nb)
        even = even_mask(nb)
        keep = lane < coarse.n
        if coarse.dist:
            q = side(coarse)
            halo_lane = lane == jnp.where(xi == 0, coarse.n, 127)
            target_lane = jnp.where(xi == 0, coarse.n, 127)
            halos = [coarse.hx[colour][...] for colour in (RED, BLACK)]

        def step(k, carry):
            parts = []
            for colour in (RED, BLACK):
                value = jnp.where(keep, coarse.v[colour][rows((k + 1) * pitch + TILE, nb), :], 0.0)
                if coarse.dist:
                    rolled = pltpu.roll(halos[colour], lax.rem(target_lane - k + LANES, LANES), 1)
                    value = jnp.where(halo_lane, rolled, value)
                parts.append(value)
            red, black = parts
            planes_ref[rows((2 * k + 1) * pitch + TILE, nb), :] = matmul(jnp.where(even, red, black), matrix)
            planes_ref[rows((2 * k + 2) * pitch + TILE, nb), :] = matmul(jnp.where(even, black, red), matrix)
            return carry
        lax.fori_loop(0, coarse.planes, step, 0)

    def negate_row(ref, src, dst):
        ref[pl.ds(dst, 1), :] = -ref[pl.ds(src, 1), :]

    def pad_local(coarse, planes_ref):
        n, pitch = coarse.n, coarse.pitch
        if n >= TILE:
            for src, dst in ((0, -1), (n - 1, n)):
                values = planes_ref[pl.ds(pitch + TILE + src, n, stride=pitch), :]
                planes_ref[pl.ds(pitch + TILE + dst, n, stride=pitch), :] = -values
        else:
            for k in range(1, n + 1):
                negate_row(planes_ref, k * pitch + TILE, k * pitch + 7)
                negate_row(planes_ref, k * pitch + TILE + n - 1, k * pitch + TILE + n)
        planes_ref[rows(0, pitch), :] = -planes_ref[rows(pitch, pitch), :]
        planes_ref[rows((n + 1) * pitch, pitch), :] = -planes_ref[rows(n * pitch, pitch), :]

    def pad_distributed(coarse, planes_ref):
        n, pitch = coarse.n, coarse.pitch
        y_own = jnp.where(yi == 0, n - 1, 0)
        y_halo = jnp.where(yi == 0, n, -1)
        z_own = jnp.where(zi == 0, n, 1)
        z_halo_mine = jnp.where(zi == 0, n + 1, 0)
        z_halo_theirs = jnp.where(zi == 0, 0, n + 1)
        refs['pfy'][...] = planes_ref[pl.ds(pitch + TILE + y_own, n, stride=pitch), :]
        copy_rows = pltpu.make_async_remote_copy(
            src_ref=refs['pfy'], dst_ref=refs['phy'], send_sem=refs['qs'].at[0], recv_sem=refs['qr'].at[0],
            device_id={'y': 1 - yi}, device_id_type=MESH)
        copy_plane = pltpu.make_async_remote_copy(
            src_ref=planes_ref.at[rows(z_own * pitch + TILE, n)], dst_ref=planes_ref.at[rows(z_halo_theirs * pitch + TILE, n)],
            send_sem=refs['qs'].at[1], recv_sem=refs['qr'].at[1],
            device_id={'z': 1 - zi}, device_id_type=MESH)
        corner = z_own * pitch + TILE + jnp.where(yi == 0, n - TILE, 0)
        copy_corner = pltpu.make_async_remote_copy(
            src_ref=planes_ref.at[rows(corner, TILE)], dst_ref=refs['phc'],
            send_sem=refs['qs'].at[2], recv_sem=refs['qr'].at[2],
            device_id={'z': 1 - zi, 'y': 1 - yi}, device_id_type=MESH)
        copy_rows.start()
        copy_plane.start()
        copy_corner.start()
        ghost_src, ghost_dst = jnp.where(yi == 0, 0, n - 1), jnp.where(yi == 0, -1, n)
        values = planes_ref[pl.ds(pitch + TILE + ghost_src, n, stride=pitch), :]
        planes_ref[pl.ds(pitch + TILE + ghost_dst, n, stride=pitch), :] = -values
        copy_rows.wait()
        planes_ref[pl.ds(pitch + TILE + y_halo, n, stride=pitch), :] = refs['phy'][...]
        copy_plane.wait()
        base = z_halo_mine * pitch + TILE
        negate_row(planes_ref, base + ghost_src, base + ghost_dst)
        copy_corner.wait()
        planes_ref[pl.ds(base + y_halo, 1), :] = refs['phc'][pl.ds(jnp.where(yi == 0, 0, 7), 1), :]
        z_edge, z_ghost = jnp.where(zi == 0, 1, n), jnp.where(zi == 0, 0, n + 1)
        planes_ref[rows(z_ghost * pitch, pitch), :] = -planes_ref[rows(z_edge * pitch, pitch), :]

    def expand_zy(coarse, planes_ref, fine, z_offset, y_offset):
        half = fine.n // 2
        size = half
        pitch = coarse.pitch
        even_lane = lax.rem(lanes(size), 2) == 0

        def step(k, carry):
            middle = (k + z_offset + 1) * pitch + TILE + y_offset
            low, high = {}, {}
            for dy in (-1, 0, 1):
                here = 0.75 * planes_ref[pl.ds(middle + dy, size), :]
                low[dy] = here + 0.25 * planes_ref[pl.ds(middle - pitch + dy, size), :]
                high[dy] = here + 0.25 * planes_ref[pl.ds(middle + pitch + dy, size), :]
            for odd in (0, 1):
                dy = 2 * odd - 1
                z_even = 0.75 * low[0] + 0.25 * low[dy]
                z_odd = 0.75 * high[0] + 0.25 * high[dy]
                first = jnp.where(even_lane, z_even, z_odd)
                second = jnp.where(even_lane, z_odd, z_even)
                red, black = (first, second) if odd == 0 else (second, first)
                span = pl.ds((k + 1) * fine.pitch + TILE + odd, size, stride=2)
                fine.v[RED][span, :] = fine.v[RED][span, :] + red
                fine.v[BLACK][span, :] = fine.v[BLACK][span, :] + black
            return carry
        lax.fori_loop(0, fine.planes, step, 0)

    barrier = pltpu.get_barrier_semaphore()
    for target in ({'x': 1 - xi}, {'y': 1 - yi}, {'z': 1 - zi}, {'z': 1 - zi, 'y': 1 - yi}):
        pl.semaphore_signal(barrier, inc=1, device_id=target, device_id_type=MESH)
    pl.semaphore_wait(barrier, 4)

    top = levels[0]
    load_chunks = 4
    chunk_rows = edge * edge // load_chunks

    def load_copy(index, which):
        span = rows(index * chunk_rows, chunk_rows)
        return pltpu.make_async_copy(
            (refs['u_in'], refs['f_in'])[which].at[span], (stage_u, stage_f)[which].at[span],
            refs['load'].at[2 * index + which])

    for index in range(load_chunks):
        for which in (0, 1):
            load_copy(index, which).start()
    even_edge = even_mask(edge)
    scale = 1.0 / float((2 * edge) ** 2)

    def pack(index, carry):
        load_copy(index, 0).wait()
        load_copy(index, 1).wait()

        def step(i, inner):
            k = index * (top.planes // load_chunks) + i
            a, b = stage_u[rows(2 * k * edge, edge), :], stage_u[rows((2 * k + 1) * edge, edge), :]
            top.v[RED][rows((k + 1) * top.pitch + TILE, edge), :] = jnp.where(even_edge, a, b)
            top.v[BLACK][rows((k + 1) * top.pitch + TILE, edge), :] = jnp.where(even_edge, b, a)
            a = stage_f[rows(2 * k * edge, edge), :] * scale
            b = stage_f[rows((2 * k + 1) * edge, edge), :] * scale
            top.g[RED][rows(k * edge, edge), :] = jnp.where(even_edge, a, b)
            top.g[BLACK][rows(k * edge, edge), :] = jnp.where(even_edge, b, a)
            return inner
        return lax.fori_loop(0, top.planes // load_chunks, step, carry)
    lax.fori_loop(0, load_chunks, pack, 0)

    for index in range(len(levels) - 1):
        refs[f'mat_q{index}'][...] = restriction_matrix(levels[index].n // 2)
    refs['mat_p0'][...] = distributed_matrix(levels[1].n)
    refs['mat_p1'][...] = prolongation_matrix(levels[1].n, levels[2].n, xi * (levels[2].n // 2), None, None)
    for index in range(2, len(levels) - 1):
        fine_n = levels[index].n
        refs[f'mat_p{index}'][...] = prolongation_matrix(fine_n, fine_n // 2, 0, None, None)

    planes_dist, planes_local = refs['planes_dist'], refs['planes_local']

    def residual(level):
        half_sweep(level, RED, 'res0')
        half_sweep(level, BLACK, 'res1')

    def start_zero(level):
        set_zero(level.v[BLACK], (level.planes + 2) * level.pitch)
        half_sweep(level, RED, 'zero')
        half_sweep(level, BLACK, 'gs')
        sweeps(level, 1)

    def solve_local(index):
        level = levels[index]
        if index == len(levels) - 1:
            set_zero(level.v[BLACK], (level.planes + 2) * level.pitch)
            half_sweep(level, RED, 'zero')
            half_sweep(level, BLACK, 'gs')
            sweeps(level, COARSE_SWEEPS - 1)
            return
        start_zero(level)
        residual(level)
        restrict_local(level, levels[index + 1], index)
        solve_local(index + 1)
        expand_x(levels[index + 1], planes_local, refs[f'mat_p{index}'][...])
        pad_local(levels[index + 1], planes_local)
        expand_zy(levels[index + 1], planes_local, level, 0, 0)
        sweeps(level, 2)

    half_sweep(top, BLACK, 'copy')

    def cycle(index, carry):
        middle = levels[1]
        sweeps(top, 2)
        residual(top)
        restrict_local(top, middle, 0)
        start_zero(middle)
        residual(middle)
        restrict_gather(levels[2])
        solve_local(2)
        expand_x(levels[2], planes_local, refs['mat_p1'][...])
        pad_local(levels[2], planes_local)
        expand_zy(levels[2], planes_local, middle, zi * (levels[2].n // 2), yi * (levels[2].n // 2))
        half_sweep(middle, BLACK, 'copy')
        sweeps(middle, 2)
        wait_all(middle, BLACK)
        expand_x(middle, planes_dist, refs['mat_p0'][...])
        pad_distributed(middle, planes_dist)
        expand_zy(middle, planes_dist, top, 0, 0)
        half_sweep(top, BLACK, 'copy')
        sweeps(top, 2)
        return carry
    lax.fori_loop(0, CYCLES, cycle, 0)
    wait_all(top, BLACK)

    def store_copy(k, colour):
        return pltpu.make_async_copy(
            top.v[colour].at[rows((k + 1) * top.pitch + TILE, edge)],
            (refs['red_out'], refs['black_out'])[colour].at[rows(k * edge, edge)], refs['store'].at[2 * k + colour])

    def store_start(k, carry):
        store_copy(k, RED).start()
        store_copy(k, BLACK).start()
        return carry

    def store_wait(k, carry):
        store_copy(k, RED).wait()
        store_copy(k, BLACK).wait()
        return carry
    lax.fori_loop(0, top.planes, store_start, 0)
    lax.fori_loop(0, top.planes, store_wait, 0)


def solve_packed(initial, source, edge):
    levels = make_levels(edge)
    names = ['u_in', 'f_in', 'red_out', 'black_out']
    scratch = []

    def add(name, shape):
        names.append(name)
        scratch.append(shape)

    for index, level in enumerate(levels):
        for key, shape in level.scratch().items():
            add(f'L{index}_{key}', shape)
    add('stage_u', pltpu.VMEM((edge * edge, LANES), F32))
    add('stage_f', pltpu.VMEM((edge * edge, LANES), F32))
    for index in range(len(levels) - 1):
        add(f'mat_p{index}', pltpu.VMEM((LANES, LANES), F32))
        add(f'mat_q{index}', pltpu.VMEM((LANES, LANES), F32))
    middle, replicated = levels[1], levels[2]
    add('planes_dist', pltpu.VMEM(((middle.n + 2) * middle.pitch, LANES), F32))
    add('planes_local', pltpu.VMEM(((replicated.n + 2) * replicated.pitch, LANES), F32))
    add('pfy', pltpu.VMEM((middle.n, LANES), F32))
    add('phy', pltpu.VMEM((middle.n, LANES), F32))
    add('phc', pltpu.VMEM((TILE, LANES), F32))
    add('qs', pltpu.SemaphoreType.DMA((3,)))
    add('qr', pltpu.SemaphoreType.DMA((3,)))
    block_n = middle.n // 2
    add('gather_own', pltpu.VMEM((4 * (block_n // 4) * block_n, LANES), F32))
    add('gather_other', pltpu.VMEM((4 * (block_n // 4) * block_n, LANES), F32))
    add('gs', pltpu.SemaphoreType.DMA((3,)))
    add('gr', pltpu.SemaphoreType.DMA((3,)))
    add('ps', pltpu.SemaphoreType.DMA((4,)))
    add('pr', pltpu.SemaphoreType.DMA((4,)))
    add('load', pltpu.SemaphoreType.DMA((TILE,)))
    add('store', pltpu.SemaphoreType.DMA((edge,)))
    half = jax.ShapeDtypeStruct((edge * edge // 2, LANES), F32)
    return pl.pallas_call(
        functools.partial(kernel_body, names, edge),
        out_shape=(half, half),
        in_specs=[pl.BlockSpec(memory_space=pl.ANY)] * 2,
        out_specs=(pl.BlockSpec(memory_space=pl.ANY),) * 2,
        scratch_shapes=scratch,
        compiler_params=pltpu.CompilerParams(collective_id=0, has_side_effects=True, vmem_limit_bytes=66000000),
        name='multigrid',
    )(initial, source)


def unpack_body(red_ref, black_ref, out_ref):
    planes = red_ref.shape[0]
    even = lax.rem(lax.broadcasted_iota(jnp.int32, (LANES, LANES), 0) + lax.broadcasted_iota(jnp.int32, (LANES, LANES), 1), 2) == 0
    for k in range(planes):
        red, black = red_ref[k], black_ref[k]
        out_ref[2 * k] = jnp.where(even, red, black)
        out_ref[2 * k + 1] = jnp.where(even, black, red)


def unpack(red, black, edge):
    step = TILE
    spec = pl.BlockSpec((step, edge, LANES), lambda i: (i, 0, 0))
    return pl.pallas_call(
        unpack_body,
        grid=(edge // 2 // step,),
        out_shape=jax.ShapeDtypeStruct((edge, edge, LANES), F32),
        in_specs=[spec, spec],
        out_specs=pl.BlockSpec((2 * step, edge, LANES), lambda i: (i, 0, 0)),
        name='unpack',
    )(red.reshape(edge // 2, edge, LANES), black.reshape(edge // 2, edge, LANES))


def solution(mesh):
    grid_spec = P(('batch', 'z'), 'y', 'x')

    def local_solve(source, initial_guess):
        edge = source.shape[0]
        red, black = solve_packed(
            initial_guess.reshape(edge * edge, edge), source.reshape(edge * edge, edge), edge)
        return unpack(red, black, edge)

    return jax.shard_map(local_solve, mesh=mesh, in_specs=(grid_spec, grid_spec), out_specs=grid_spec, check_vma=False)
```

time: 8200 us -> 542 us (0.07)
  local copies, waits for them, and re-layouts: 3060 us -> 0 us
  starting transfers between devices: 2960 us -> 0 us
  other arithmetic: 1680 us -> 0 us
  Pallas kernels: 0 us -> 541 us
  waiting for transfers between devices: 429 us -> 0 us
    ppermute x1266 -> x0, starting transfers between devices: 2960 us -> none  [the longest x633 2140 us: halo_planes(): from_below = lax.ppermute(last, axis_name, upward)]
    reshape x26 -> x0, local copies, waits for them, and re-layouts: 1280 us -> none  [the longest x12 1240 us: restrict(): grid.reshape(grid_shape[0] // 2, 2, grid_shape[1] // 2, 2, grid_shape[2]...]
    slice x1003 -> x0, local copies, waits for them, and re-layouts: 1170 us -> none  [the longest x294 515 us: shifted(): lax.slice_in_dim(grid, 1, extent, axis=axis)]
    select_n x842 -> x0, other arithmetic: 1110 us -> none  [the longest x321 421 us: halo_planes(): upper = jnp.where(position == count - 1, -last, from_above)]
    pallas_call x0 -> x2, Pallas kernels: none -> 541 us  [the longest x1 532 us: solve_packed(): pl.pallas_call(functools.partial(kernel_body, names, edge), out_shape=(ha...]
    ppermute x1266 -> x0, waiting for transfers between devices: 429 us -> none  [the longest x633 426 us: halo_planes(): from_above = lax.ppermute(first, axis_name, downward)]
    reduce_sum x12 -> x0, other arithmetic: 378 us -> none  [restrict(): return folded.mean(axis=(1, 3, 5))]
    ppermute x74 -> x0, local copies, waits for them, and re-layouts: 351 us -> none  [the longest x37 176 us: halo_planes(): from_below = lax.ppermute(last, axis_name, upward)]
where the time goes in v1:
time: 542 us; the launch traced here: 541 us
  Pallas kernels  541 us (100%)
    pallas_call x1, Pallas kernels, solve_packed(): pl.pallas_call(functools.partial(kernel_body, names, edge), out_shape=(ha...  532 us

profile of v1, /device:TPU:0, one launch (start us, length us, event | category | flops | bytes accessed | tf_op | source)
XLA Modules:
  0.0 541.3 jit_solution(7682303922573838952)
XLA Ops:
  0.0 532.4 %multigrid.1 = (f32[8192,128]{1,0:T(8,128)}, f32[8192,128]{1,0:T(8,128)}) custom-call(f32[16384,128]{1,0:T(8,128)} %bitcast.4, f32[16384,128]{1,0:T(8,128)} %bitcast.5), custom_call_target="tpu_custom_call" | custom-call | tf_op jit(solution)/shard_map/multigrid/pallas_call | solution.py:633
  532.4 8.9 %unpack.1 = f32[128,128,128]{2,1,0:T(8,128)} custom-call(f32[64,128,128]{2,1,0:T(8,128)} %bitcast.6, f32[64,128,128]{2,1,0:T(8,128)} %bitcast.7), custom_call_target="tpu_custom_call" | custom-call | tf_op jit(solution)/shard_map/unpack/pallas_call | solution.py:656

commit v2 on v1

--- a/solution.py
+++ b/solution.py
@@ -10,6 +10,8 @@
 CYCLES = 2
 COARSE_SWEEPS = 24
 LANES = 128
+WIDTH = 32
+GROUP = 4
 TILE = 8
 MESH = pl.DeviceIdType.MESH
 F32 = jnp.float32
@@ -68,10 +70,10 @@
 
 
 def make_levels(edge):
-    levels = [Level(edge, True, 32, 4), Level(edge // 2, True, 32, 4)]
+    levels = [Level(edge, True, WIDTH, 16), Level(edge // 2, True, WIDTH, 8)]
     n = edge // 2
     while n >= 4:
-        levels.append(Level(n, False, 32, 4))
+        levels.append(Level(n, False, 2 * WIDTH, 8))
         n = n // 2
     return levels
 
@@ -92,6 +94,12 @@
 
     def side(level):
         return jnp.where(xi == 0, level.n - 1, 0)
+
+    def turn(value, shift):
+        return pltpu.roll(value, lax.rem(shift + 2 * LANES, LANES), 1)
+
+    def skew(level, k):
+        return k + level.planes * zi if level.dist else k
 
     def copy_x(level, colour, j):
         span = rows(j * level.width, level.width)
@@ -131,6 +139,8 @@
             return carry
         lax.fori_loop(0, level.chunks, step, 0)
 
+    stage_u, stage_f = refs['stage_u'], refs['stage_f']
+
     def fill_ghosts(level, colour):
         own, other = level.v[colour], level.v[1 - colour]
         pitch, n = level.pitch, level.n
@@ -144,17 +154,11 @@
                     base = (k + 1) * pitch + TILE
                     other[pl.ds(base + dst, 1), :] = -own[pl.ds(base + src, 1), :]
 
-        def fill_plane(src, dst):
-            other[rows(dst * pitch + TILE, level.nb), :] = -own[rows(src * pitch + TILE, level.nb), :]
-
         if level.dist:
             fill_row(jnp.where(yi == 0, 0, n - 1), jnp.where(yi == 0, -1, n))
-            fill_plane(jnp.where(zi == 0, 1, level.planes), jnp.where(zi == 0, 0, level.planes + 1))
         else:
             fill_row(0, -1)
             fill_row(n - 1, n)
-            fill_plane(1, 0)
-            fill_plane(level.planes, level.planes + 1)
 
     def half_sweep(level, colour, mode):
         own, other, source = level.v[colour], level.v[1 - colour], level.g[colour]
@@ -168,11 +172,9 @@
             wait_y(level, 1 - colour)
         lane = lanes(width)
         even = even_mask(width)
-        takes_below = even if colour == RED else jnp.logical_not(even)
-        first_lane, last_lane = lane == 0, lane == n - 1
-        if level.dist:
-            q = side(level)
-            halo_lane = lane == q
+        odd = jnp.logical_not(even)
+        takes_below = (even, odd) if colour == RED else (odd, even)
+        q = side(level)
 
         def chunk(jj, carry):
             j = jnp.where(yi == 1, jj, level.chunks - 1 - jj) if level.dist else jj
@@ -180,52 +182,92 @@
                 copy_x(level, 1 - colour, j).wait()
                 copy_z(level, 1 - colour, j).wait()
             row0 = j * width + TILE
+            blank = jnp.zeros((width, LANES), F32)
+            unroll = level.unroll
+            steps = planes // unroll
+            pair_sum = refs['pair_sum']
             if stencil and level.dist:
                 halo = level.hx[1 - colour][rows(j * width, width), :]
 
-            def planes_step(i, state):
-                below, here, face = state
-                for u in range(level.unroll):
-                    k = i * level.unroll + u
-                    base = (k + 1) * pitch + row0
-                    if mode != 'zero':
-                        old = own[rows(base, width), :]
+            def load(ref, start):
+                return ref[rows(start, width), :]
+
+            def turned(start):
+                here = load(other, start)
+                return pltpu.roll(here, 1, 1), pltpu.roll(here, LANES - 1, 1)
+
+            def ghost(start, rotated, outside):
+                minus = -load(own, start)
+                return minus if rotated is None else jnp.where(outside, minus, rotated)
+
+            def at(place):
+                return lane == lax.rem(place, LANES)
+
+            def along_x(start, place, left, right):
+                ends = -load(own, start)
+                if level.dist:
+                    ends = lax.select(at(place + q), halo, ends)
+                return lax.select(at(place), ends, left) + lax.select(at(place + (n - 1)), ends, right)
+
+            def across(i, state):
+                older, newer, sums = state
+                start = (i * unroll + 1) * pitch + row0
+                place = skew(level, i * unroll)
+                final = i == steps - 1
+                for u in range(unroll):
+                    left, right = turned(start + (u + 1) * pitch)
+                    following = start + (u + 1) * pitch
+                    if u == unroll - 1:
+                        outside = final & (zi == 1) if level.dist else final
+                        right = ghost(start + u * pitch, right, outside)
+                        following = start + jnp.where(final, u, u + 1) * pitch
+                    sums = sums + lax.select(takes_below[u % 2], older, right)
+                    pair_sum[rows(i * (unroll * width) + u * width, width), :] = sums
+                    older, newer, sums = newer, left, along_x(following, place + (u + 1), left, right)
+                return older, newer, sums
+
+            def update(i, face):
+                start = (i * unroll + 1) * pitch + row0
+                place = skew(level, i * unroll) + q
+                packed = i * (unroll * level.nb) + j * width
+                for u in range(unroll):
+                    base = start + u * pitch
+                    span = rows(packed + u * level.nb, width)
                     if mode == 'copy':
-                        new = old
+                        new = load(own, base)
                     elif mode == 'zero':
-                        new = source[rows(k * level.nb + j * width, width), :] * SIXTH
+                        new = source[span, :] * SIXTH
                     else:
-                        above = other[rows(base + pitch, width), :]
                         total = other[pl.ds(base - 1, width), :] + other[pl.ds(base + 1, width), :]
-                        edge_values = -old
-                        if level.dist:
-                            shift = lax.rem(q - k + LANES, LANES)
-                            edge_values = jnp.where(halo_lane, pltpu.roll(halo, shift, 1), edge_values)
-                        left = jnp.where(first_lane, edge_values, pltpu.roll(here, 1, 1))
-                        right = jnp.where(last_lane, edge_values, pltpu.roll(here, 127, 1))
-                        total = total + (left + right) + (here + jnp.where(takes_below, below, above))
-                        total = total + source[rows(k * level.nb + j * width, width), :]
-                        new = total * SIXTH if mode == 'gs' else total - 6.0 * old
-                        below, here = here, above
+                        total = total + load(pair_sum, i * (unroll * width) + u * width)
+                        total = total + load(other, base) + source[span, :]
+                        new = total * SIXTH if mode == 'gs' else total - 6.0 * load(own, base)
                     if mode in ('gs', 'zero'):
                         own[rows(base, width), :] = new
                     elif mode == 'res0':
-                        refs['stage_u'][rows(k * level.nb + j * width, width), :] = new
+                        stage_u[span, :] = new
                     elif mode == 'res1':
-                        span = rows(k * level.nb + j * width, width)
-                        refs['stage_u'][span, :] = refs['stage_u'][span, :] + new
+                        stage_u[span, :] = stage_u[span, :] + new
                     if sends:
-                        face = jnp.where(lane == k, pltpu.roll(new, lax.rem(k - q + LANES, LANES), 1), face)
-                return below, here, face
-
-            blank = jnp.zeros((width, LANES), F32)
+                        face = lax.select(at(place + u), new, face)
+                return face
+
             if stencil:
-                start = (other[rows(row0, width), :], other[rows(pitch + row0, width), :], blank)
+                first = pitch + row0
+                below = ghost(first, turned(row0)[0] if level.dist else None, zi == 0)
+                left, right = turned(first)
+                state = across(0, (below, left, along_x(first, skew(level, 0), left, right)))
+
+                def planes_step(i, carried):
+                    state, face = carried
+                    state = across(i + 1, state)
+                    return state, update(i, face)
+                _, face = lax.fori_loop(0, steps - 1, planes_step, (state, blank))
+                face = update(steps - 1, face)
             else:
-                start = (blank, blank, blank)
-            _, _, face = lax.fori_loop(0, planes // level.unroll, planes_step, start)
+                face = lax.fori_loop(0, steps, update, blank)
             if sends:
-                level.fx[colour][rows(j * width, width), :] = face
+                level.fx[colour][rows(j * width, width), :] = turn(face, (2 * xi - 1) * (n - 1))
                 copy_x(level, colour, j).start()
                 copy_z(level, colour, j).start()
 
@@ -274,8 +316,6 @@
     def matmul(a, b):
         return jnp.dot(a, b, precision=HIGHEST, preferred_element_type=F32)
 
-    stage_u, stage_f = refs['stage_u'], refs['stage_f']
-
     def restrict_pair(level, k, matrix):
         n_coarse = level.n // 2
         size = max(n_coarse, TILE)
@@ -283,19 +323,28 @@
         for z in (0, 1):
             base = (2 * k + z) * level.nb
             total = stage_u[pl.ds(base, size, stride=2), :] + stage_u[pl.ds(base + 1, size, stride=2), :]
-            pair.append(matmul(total, matrix))
+            pair.append(matmul(turn(total, -skew(level, 2 * k + z)), matrix))
         even = even_mask(size)
         return jnp.where(even, pair[0], pair[1]), jnp.where(even, pair[1], pair[0])
 
+    def grouped(count, size, body):
+        size = min(size, count)
+
+        def step(i, carry):
+            body([i * size + u for u in range(size)])
+            return carry
+        lax.fori_loop(0, count // size, step, 0)
+
     def restrict_local(level, coarse, index):
         matrix = refs[f'mat_q{index}'][...]
 
-        def step(k, carry):
-            red, black = restrict_pair(level, k, matrix)
-            coarse.g[RED][rows(k * coarse.nb, coarse.nb), :] = red
-            coarse.g[BLACK][rows(k * coarse.nb, coarse.nb), :] = black
-            return carry
-        lax.fori_loop(0, coarse.planes, step, 0)
+        def step(indices):
+            pairs = [restrict_pair(level, k, matrix) for k in indices]
+            pairs = [[turn(part, skew(coarse, k)) for part in pair] for k, pair in zip(indices, pairs)]
+            for k, pair in zip(indices, pairs):
+                for colour in (RED, BLACK):
+                    coarse.g[colour][rows(k * coarse.nb, coarse.nb), :] = pair[colour]
+        grouped(coarse.planes, GROUP, step)
 
     gather_own, gather_other = refs['gather_own'], refs['gather_other']
     fine_block = levels[1]
@@ -326,16 +375,15 @@
     def restrict_gather(coarse):
         matrix = refs['mat_q1'][...]
 
-        def step(m, carry):
-            packed = None
-            for half in (0, 1):
-                for colour, part in enumerate(restrict_pair(fine_block, 2 * m + half, matrix)):
-                    turn = (2 * half + colour) * block_n
-                    part = part if turn == 0 else pltpu.roll(part, turn, 1)
-                    packed = part if packed is None else packed + part
-            gather_own[rows(slot * block_rows + m * block_n, block_n), :] = packed
-            return carry
-        lax.fori_loop(0, block_n // 4, step, 0)
+        def step(indices):
+            for m in indices:
+                packed = None
+                for half in (0, 1):
+                    for colour, part in enumerate(restrict_pair(fine_block, 2 * m + half, matrix)):
+                        part = turn(part, (2 * half + colour) * block_n)
+                        packed = part if packed is None else packed + part
+                gather_own[rows(slot * block_rows + m * block_n, block_n), :] = packed
+        grouped(block_n // 4, GROUP, step)
         copies = gather_copies()
         for copy in copies:
             copy.start()
@@ -346,26 +394,28 @@
         for index in range(4):
             partner_copy(index).wait()
         lane = lanes(block_n)
-        low, middle = lane < block_n, lane < 2 * block_n
 
         for source_slot in range(4):
             zs, ys = source_slot // 2, source_slot % 2
 
-            def unpack(m, carry):
-                span = rows(source_slot * block_rows + m * block_n, block_n)
-                mine, theirs = gather_own[span, :], gather_other[span, :]
-                at_zero = jnp.where(xi == 0, mine, theirs)
-                at_one = jnp.where(xi == 0, theirs, mine)
-                for group in range(4):
-                    half, colour = group // 2, group % 2
-                    left = at_zero if group == 0 else pltpu.roll(at_zero, LANES - group * block_n, 1)
-                    turn = (LANES - group * block_n + block_n) % LANES
-                    right = at_one if turn == 0 else pltpu.roll(at_one, turn, 1)
-                    value = jnp.where(low, left, jnp.where(middle, right, 0.0))
-                    plane = zs * (block_n // 2) + 2 * m + half
+            def unpack(indices):
+                results = []
+                for m in indices:
+                    span = rows(source_slot * block_rows + m * block_n, block_n)
+                    mine, theirs = gather_own[span, :], gather_other[span, :]
+                    at_zero = jnp.where(xi == 0, mine, theirs)
+                    at_one = jnp.where(xi == 0, theirs, mine)
+                    for group in range(4):
+                        half, colour = group // 2, group % 2
+                        plane = zs * (block_n // 2) + 2 * m + half
+                        left = turn(at_zero, plane - group * block_n)
+                        right = turn(at_one, plane + block_n - group * block_n)
+                        place = lax.rem(lane + LANES - plane, LANES)
+                        value = jnp.where(place < block_n, left, jnp.where(place < 2 * block_n, right, 0.0))
+                        results.append((colour, plane, value))
+                for colour, plane, value in results:
                     coarse.g[colour][rows(plane * coarse.nb + ys * block_n, block_n), :] = value
-                return carry
-            lax.fori_loop(0, block_n // 4, unpack, 0)
+            grouped(block_n // 4, GROUP, unpack)
 
     def set_zero(ref, size):
         def step(i, carry):
@@ -384,19 +434,23 @@
             target_lane = jnp.where(xi == 0, coarse.n, 127)
             halos = [coarse.hx[colour][...] for colour in (RED, BLACK)]
 
-        def step(k, carry):
-            parts = []
-            for colour in (RED, BLACK):
-                value = jnp.where(keep, coarse.v[colour][rows((k + 1) * pitch + TILE, nb), :], 0.0)
-                if coarse.dist:
-                    rolled = pltpu.roll(halos[colour], lax.rem(target_lane - k + LANES, LANES), 1)
-                    value = jnp.where(halo_lane, rolled, value)
-                parts.append(value)
-            red, black = parts
-            planes_ref[rows((2 * k + 1) * pitch + TILE, nb), :] = matmul(jnp.where(even, red, black), matrix)
-            planes_ref[rows((2 * k + 2) * pitch + TILE, nb), :] = matmul(jnp.where(even, black, red), matrix)
-            return carry
-        lax.fori_loop(0, coarse.planes, step, 0)
+        def step(indices):
+            results = []
+            for k in indices:
+                parts = []
+                for colour in (RED, BLACK):
+                    value = turn(coarse.v[colour][rows((k + 1) * pitch + TILE, nb), :], -skew(coarse, k))
+                    value = jnp.where(keep, value, 0.0)
+                    if coarse.dist:
+                        halo = turn(halos[colour], target_lane - q - skew(coarse, k))
+                        value = jnp.where(halo_lane, halo, value)
+                    parts.append(value)
+                red, black = parts
+                results.append(matmul(jnp.where(even, red, black), matrix))
+                results.append(matmul(jnp.where(even, black, red), matrix))
+            for offset, value in enumerate(results):
+                planes_ref[rows((2 * indices[0] + 1 + offset) * pitch + TILE, nb), :] = value
+        grouped(coarse.planes, GROUP, step)
 
     def negate_row(ref, src, dst):
         ref[pl.ds(dst, 1), :] = -ref[pl.ds(src, 1), :]
@@ -456,25 +510,27 @@
         pitch = coarse.pitch
         even_lane = lax.rem(lanes(size), 2) == 0
 
-        def step(k, carry):
-            middle = (k + z_offset + 1) * pitch + TILE + y_offset
-            low, high = {}, {}
-            for dy in (-1, 0, 1):
-                here = 0.75 * planes_ref[pl.ds(middle + dy, size), :]
-                low[dy] = here + 0.25 * planes_ref[pl.ds(middle - pitch + dy, size), :]
-                high[dy] = here + 0.25 * planes_ref[pl.ds(middle + pitch + dy, size), :]
-            for odd in (0, 1):
-                dy = 2 * odd - 1
-                z_even = 0.75 * low[0] + 0.25 * low[dy]
-                z_odd = 0.75 * high[0] + 0.25 * high[dy]
-                first = jnp.where(even_lane, z_even, z_odd)
-                second = jnp.where(even_lane, z_odd, z_even)
-                red, black = (first, second) if odd == 0 else (second, first)
-                span = pl.ds((k + 1) * fine.pitch + TILE + odd, size, stride=2)
-                fine.v[RED][span, :] = fine.v[RED][span, :] + red
-                fine.v[BLACK][span, :] = fine.v[BLACK][span, :] + black
-            return carry
-        lax.fori_loop(0, fine.planes, step, 0)
+        def step(indices):
+            results = []
+            for k in indices:
+                middle = (k + z_offset + 1) * pitch + TILE + y_offset
+                low, high = {}, {}
+                for dy in (-1, 0, 1):
+                    here = 0.75 * planes_ref[pl.ds(middle + dy, size), :]
+                    low[dy] = here + 0.25 * planes_ref[pl.ds(middle - pitch + dy, size), :]
+                    high[dy] = here + 0.25 * planes_ref[pl.ds(middle + pitch + dy, size), :]
+                for odd in (0, 1):
+                    dy = 2 * odd - 1
+                    z_even = 0.75 * low[0] + 0.25 * low[dy]
+                    z_odd = 0.75 * high[0] + 0.25 * high[dy]
+                    first = turn(jnp.where(even_lane, z_even, z_odd), skew(fine, k))
+                    second = turn(jnp.where(even_lane, z_odd, z_even), skew(fine, k))
+                    span = pl.ds((k + 1) * fine.pitch + TILE + odd, size, stride=2)
+                    for colour, change in ((odd, first), (1 - odd, second)):
+                        results.append((colour, span, fine.v[colour][span, :] + change))
+            for colour, span, value in results:
+                fine.v[colour][span, :] = value
+        grouped(fine.planes, 2, step)
 
     barrier = pltpu.get_barrier_semaphore()
     for target in ({'x': 1 - xi}, {'y': 1 - yi}, {'z': 1 - zi}, {'z': 1 - zi, 'y': 1 - yi}):
@@ -504,12 +560,12 @@
         def step(i, inner):
             k = index * (top.planes // load_chunks) + i
             a, b = stage_u[rows(2 * k * edge, edge), :], stage_u[rows((2 * k + 1) * edge, edge), :]
-            top.v[RED][rows((k + 1) * top.pitch + TILE, edge), :] = jnp.where(even_edge, a, b)
-            top.v[BLACK][rows((k + 1) * top.pitch + TILE, edge), :] = jnp.where(even_edge, b, a)
+            top.v[RED][rows((k + 1) * top.pitch + TILE, edge), :] = turn(jnp.where(even_edge, a, b), skew(top, k))
+            top.v[BLACK][rows((k + 1) * top.pitch + TILE, edge), :] = turn(jnp.where(even_edge, b, a), skew(top, k))
             a = stage_f[rows(2 * k * edge, edge), :] * scale
             b = stage_f[rows((2 * k + 1) * edge, edge), :] * scale
-            top.g[RED][rows(k * edge, edge), :] = jnp.where(even_edge, a, b)
-            top.g[BLACK][rows(k * edge, edge), :] = jnp.where(even_edge, b, a)
+            top.g[RED][rows(k * edge, edge), :] = turn(jnp.where(even_edge, a, b), skew(top, k))
+            top.g[BLACK][rows(k * edge, edge), :] = turn(jnp.where(even_edge, b, a), skew(top, k))
             return inner
         return lax.fori_loop(0, top.planes // load_chunks, step, carry)
     lax.fori_loop(0, load_chunks, pack, 0)
@@ -528,53 +584,71 @@
         half_sweep(level, RED, 'res0')
         half_sweep(level, BLACK, 'res1')
 
-    def start_zero(level):
-        set_zero(level.v[BLACK], (level.planes + 2) * level.pitch)
-        half_sweep(level, RED, 'zero')
-        half_sweep(level, BLACK, 'gs')
-        sweeps(level, 1)
+    def solve(level, sweep_count, phases, descend):
+        def phase(p, carry):
+            def sweep(index, inner):
+                fresh = (p == 0) & (index == 0)
+
+                @pl.when(fresh)
+                def _():
+                    set_zero(level.v[BLACK], (level.planes + 2) * level.pitch)
+                    half_sweep(level, RED, 'zero')
+
+                @pl.when(jnp.logical_not(fresh))
+                def _():
+                    half_sweep(level, RED, 'gs')
+                half_sweep(level, BLACK, 'gs')
+                return inner
+            lax.fori_loop(0, sweep_count, sweep, 0)
+            if phases == 2:
+                @pl.when(p == 0)
+                def _():
+                    residual(level)
+                    descend()
+            return carry
+        lax.fori_loop(0, phases, phase, 0)
 
     def solve_local(index):
         level = levels[index]
         if index == len(levels) - 1:
-            set_zero(level.v[BLACK], (level.planes + 2) * level.pitch)
-            half_sweep(level, RED, 'zero')
-            half_sweep(level, BLACK, 'gs')
-            sweeps(level, COARSE_SWEEPS - 1)
+            solve(level, COARSE_SWEEPS, 1, None)
             return
-        start_zero(level)
-        residual(level)
-        restrict_local(level, levels[index + 1], index)
-        solve_local(index + 1)
-        expand_x(levels[index + 1], planes_local, refs[f'mat_p{index}'][...])
-        pad_local(levels[index + 1], planes_local)
-        expand_zy(levels[index + 1], planes_local, level, 0, 0)
-        sweeps(level, 2)
+
+        def descend():
+            restrict_local(level, levels[index + 1], index)
+            solve_local(index + 1)
+            expand_x(levels[index + 1], planes_local, refs[f'mat_p{index}'][...])
+            pad_local(levels[index + 1], planes_local)
+            expand_zy(levels[index + 1], planes_local, level, 0, 0)
+        solve(level, 2, 2, descend)
+
+    middle, replicated = levels[1], levels[2]
+
+    def descend_middle():
+        restrict_gather(replicated)
+        solve_local(2)
+        expand_x(replicated, planes_local, refs['mat_p1'][...])
+        pad_local(replicated, planes_local)
+        expand_zy(replicated, planes_local, middle, zi * (replicated.n // 2), yi * (replicated.n // 2))
+        half_sweep(middle, BLACK, 'copy')
 
     half_sweep(top, BLACK, 'copy')
 
-    def cycle(index, carry):
-        middle = levels[1]
+    def sweep_pair(index, carry):
         sweeps(top, 2)
-        residual(top)
-        restrict_local(top, middle, 0)
-        start_zero(middle)
-        residual(middle)
-        restrict_gather(levels[2])
-        solve_local(2)
-        expand_x(levels[2], planes_local, refs['mat_p1'][...])
-        pad_local(levels[2], planes_local)
-        expand_zy(levels[2], planes_local, middle, zi * (levels[2].n // 2), yi * (levels[2].n // 2))
-        half_sweep(middle, BLACK, 'copy')
-        sweeps(middle, 2)
-        wait_all(middle, BLACK)
-        expand_x(middle, planes_dist, refs['mat_p0'][...])
-        pad_distributed(middle, planes_dist)
-        expand_zy(middle, planes_dist, top, 0, 0)
-        half_sweep(top, BLACK, 'copy')
-        sweeps(top, 2)
+
+        @pl.when(lax.rem(index, 2) == 0)
+        def _():
+            residual(top)
+            restrict_local(top, middle, 0)
+            solve(middle, 2, 2, descend_middle)
+            wait_all(middle, BLACK)
+            expand_x(middle, planes_dist, refs['mat_p0'][...])
+            pad_distributed(middle, planes_dist)
+            expand_zy(middle, planes_dist, top, 0, 0)
+            half_sweep(top, BLACK, 'copy')
         return carry
-    lax.fori_loop(0, CYCLES, cycle, 0)
+    lax.fori_loop(0, 2 * CYCLES, sweep_pair, 0)
     wait_all(top, BLACK)
 
     def store_copy(k, colour):
@@ -609,6 +683,7 @@
             add(f'L{index}_{key}', shape)
     add('stage_u', pltpu.VMEM((edge * edge, LANES), F32))
     add('stage_f', pltpu.VMEM((edge * edge, LANES), F32))
+    add('pair_sum', pltpu.VMEM((edge * WIDTH, LANES), F32))
     for index in range(len(levels) - 1):
         add(f'mat_p{index}', pltpu.VMEM((LANES, LANES), F32))
         add(f'mat_q{index}', pltpu.VMEM((LANES, LANES), F32))
@@ -643,9 +718,11 @@
 
 def unpack_body(red_ref, black_ref, out_ref):
     planes = red_ref.shape[0]
+    first = pl.program_id(0) * planes + lax.axis_index('z') * (planes * pl.num_programs(0))
     even = lax.rem(lax.broadcasted_iota(jnp.int32, (LANES, LANES), 0) + lax.broadcasted_iota(jnp.int32, (LANES, LANES), 1), 2) == 0
     for k in range(planes):
-        red, black = red_ref[k], black_ref[k]
+        shift = lax.rem(2 * LANES - first - k, LANES)
+        red, black = pltpu.roll(red_ref[k], shift, 1), pltpu.roll(black_ref[k], shift, 1)
         out_ref[2 * k] = jnp.where(even, red, black)
         out_ref[2 * k + 1] = jnp.where(even, black, red)
 

time: 542 us -> 335 us (0.62)
  Pallas kernels: 541 us -> 335 us
    pallas_call x1, Pallas kernels: 532 us -> 325 us  [solve_packed(): pl.pallas_call(functools.partial(kernel_body, names, edge), out_shape=(ha...]
where the time goes in v2:
time: 335 us
  Pallas kernels  335 us (100%)
    pallas_call x1, Pallas kernels, solve_packed(): pl.pallas_call(functools.partial(kernel_body, names, edge), out_shape=(ha...  325 us
    pallas_call x1, Pallas kernels, unpack(): pl.pallas_call(unpack_body, grid=(edge // 2 // step,), out_shape=jax.Shap...  9.84 us

profile of v2, /device:TPU:0, one launch (start us, length us, event | category | flops | bytes accessed | tf_op | source)
XLA Modules:
  0.0 334.8 jit_solution(16458919747135915824)
XLA Ops:
  0.0 325.0 %multigrid.1 = (f32[8192,128]{1,0:T(8,128)}, f32[8192,128]{1,0:T(8,128)}) custom-call(f32[16384,128]{1,0:T(8,128)} %bitcast.4, f32[16384,128]{1,0:T(8,128)} %bitcast.5), custom_call_target="tpu_custom_call" | custom-call | tf_op jit(solution)/shard_map/multigrid/pallas_call | solution.py:708
  325.0 9.8 %unpack.1 = f32[128,128,128]{2,1,0:T(8,128)} custom-call(f32[64,128,128]{2,1,0:T(8,128)} %bitcast.6, f32[64,128,128]{2,1,0:T(8,128)} %bitcast.7), custom_call_target="tpu_custom_call" | custom-call | tf_op jit(solution)/shard_map/unpack/pallas_call | solution.py:733

commit v3 on v2

--- a/solution.py
+++ b/solution.py
@@ -11,7 +11,7 @@
 COARSE_SWEEPS = 24
 LANES = 128
 WIDTH = 32
-GROUP = 4
+GROUP = 8
 TILE = 8
 MESH = pl.DeviceIdType.MESH
 F32 = jnp.float32
@@ -70,10 +70,10 @@
 
 
 def make_levels(edge):
-    levels = [Level(edge, True, WIDTH, 16), Level(edge // 2, True, WIDTH, 8)]
+    levels = [Level(edge, True, WIDTH, 16), Level(edge // 2, True, WIDTH // 2, 16)]
     n = edge // 2
     while n >= 4:
-        levels.append(Level(n, False, 2 * WIDTH, 8))
+        levels.append(Level(n, False, 2 * WIDTH, 16))
         n = n // 2
     return levels
 
@@ -189,74 +189,99 @@
             if stencil and level.dist:
                 halo = level.hx[1 - colour][rows(j * width, width), :]
 
-            def load(ref, start):
-                return ref[rows(start, width), :]
-
-            def turned(start):
-                here = load(other, start)
+            reach = (unroll - 1) * pitch + width
+
+            def block(ref, start):
+                return ref[pl.ds(start, reach), :]
+
+            def cut(values, start):
+                return lax.slice(values, (start, 0), (start + width, LANES))
+
+            def turned(here):
                 return pltpu.roll(here, 1, 1), pltpu.roll(here, LANES - 1, 1)
 
-            def ghost(start, rotated, outside):
-                minus = -load(own, start)
-                return minus if rotated is None else jnp.where(outside, minus, rotated)
-
-            def at(place):
-                return lane == lax.rem(place, LANES)
-
-            def along_x(start, place, left, right):
-                ends = -load(own, start)
+            def ghost(plane, rotated, outside):
+                return -plane if rotated is None else jnp.where(outside, -plane, rotated)
+
+            def distance(place):
+                return lax.bitwise_and(lane + (2 * LANES - place), LANES - 1)
+
+            def along_x(old, u, place, face_place, left, right):
+                ends = -old
                 if level.dist:
-                    ends = lax.select(at(place + q), halo, ends)
-                return lax.select(at(place), ends, left) + lax.select(at(place + (n - 1)), ends, right)
+                    ends = lax.select(face_place == u, halo, ends)
+                left = lax.select(place == u, ends, left)
+                return left + lax.select(place == (u + n - 1) % LANES, ends, right)
 
             def across(i, state):
                 older, newer, sums = state
-                start = (i * unroll + 1) * pitch + row0
-                place = skew(level, i * unroll)
+                start = mult8((i * unroll + 1) * pitch + row0)
+                theirs = other[pl.ds(mult8(start + pitch), reach - pitch), :]
+                mine = block(own, start)
+                store = pair_sum.at[rows(i * (unroll * width), unroll * width)]
+                place = distance(skew(level, i * unroll))
+                face_place = distance(skew(level, i * unroll) + q)
                 final = i == steps - 1
+                old = cut(mine, 0)
                 for u in range(unroll):
-                    left, right = turned(start + (u + 1) * pitch)
-                    following = start + (u + 1) * pitch
-                    if u == unroll - 1:
+                    previous = old
+                    if u < unroll - 1:
+                        left, right = turned(cut(theirs, u * pitch))
+                    else:
+                        left, right = turned(other[rows(start + unroll * pitch, width), :])
+                    if u < unroll - 1:
+                        old = cut(mine, (u + 1) * pitch)
+                    else:
                         outside = final & (zi == 1) if level.dist else final
-                        right = ghost(start + u * pitch, right, outside)
-                        following = start + jnp.where(final, u, u + 1) * pitch
+                        right = ghost(previous, right, outside)
+                        old = own[rows(start + jnp.where(final, u, unroll) * pitch, width), :]
                     sums = sums + lax.select(takes_below[u % 2], older, right)
-                    pair_sum[rows(i * (unroll * width) + u * width, width), :] = sums
-                    older, newer, sums = newer, left, along_x(following, place + (u + 1), left, right)
+                    store[u * width:(u + 1) * width, :] = sums
+                    older, newer, sums = newer, left, along_x(old, u + 1, place, face_place, left, right)
                 return older, newer, sums
 
             def update(i, face):
-                start = (i * unroll + 1) * pitch + row0
-                place = skew(level, i * unroll) + q
-                packed = i * (unroll * level.nb) + j * width
+                start = mult8((i * unroll + 1) * pitch + row0)
+                mine = own.at[pl.ds(start, reach)]
+                packed = rows(i * (unroll * level.nb) + j * width, (unroll - 1) * level.nb + width)
+                stage = stage_u.at[packed]
+                face_place = distance(skew(level, i * unroll) + q)
+                if mode != 'copy':
+                    scaled = source[packed, :]
+                if mode != 'zero' and mode != 'gs':
+                    old = block(own, start)
+                if stencil:
+                    here, before, after = block(other, start), block(other, start - 1), block(other, start + 1)
+                    across_sums = pair_sum[rows(i * (unroll * width), unroll * width), :]
+                if mode == 'res1':
+                    staged = stage[...]
                 for u in range(unroll):
-                    base = start + u * pitch
-                    span = rows(packed + u * level.nb, width)
+                    base, line = u * pitch, u * level.nb
                     if mode == 'copy':
-                        new = load(own, base)
+                        new = cut(old, base)
                     elif mode == 'zero':
-                        new = source[span, :] * SIXTH
+                        new = cut(scaled, line) * SIXTH
                     else:
-                        total = other[pl.ds(base - 1, width), :] + other[pl.ds(base + 1, width), :]
-                        total = total + load(pair_sum, i * (unroll * width) + u * width)
-                        total = total + load(other, base) + source[span, :]
-                        new = total * SIXTH if mode == 'gs' else total - 6.0 * load(own, base)
+                        total = cut(before, base) + cut(after, base) + cut(across_sums, u * width)
+                        total = total + cut(here, base) + cut(scaled, line)
+                        new = total * SIXTH if mode == 'gs' else total - 6.0 * cut(old, base)
                     if mode in ('gs', 'zero'):
-                        own[rows(base, width), :] = new
+                        mine[base:base + width, :] = new
                     elif mode == 'res0':
-                        stage_u[span, :] = new
+                        stage[line:line + width, :] = new
                     elif mode == 'res1':
-                        stage_u[span, :] = stage_u[span, :] + new
+                        stage[line:line + width, :] = cut(staged, line) + new
                     if sends:
-                        face = lax.select(at(place + u), new, face)
+                        face = lax.select(face_place == u, new, face)
                 return face
 
             if stencil:
-                first = pitch + row0
-                below = ghost(first, turned(row0)[0] if level.dist else None, zi == 0)
-                left, right = turned(first)
-                state = across(0, (below, left, along_x(first, skew(level, 0), left, right)))
+                first = own[rows(pitch + row0, width), :]
+                below = turned(other[rows(row0, width), :])[0] if level.dist else None
+                below = ghost(first, below, zi == 0)
+                left, right = turned(other[rows(pitch + row0, width), :])
+                place = skew(level, 0)
+                state = across(0, (below, left, along_x(first, 0, distance(place), distance(place + q), left, right)))
 
                 def planes_step(i, carried):
                     state, face = carried
@@ -395,8 +420,8 @@
             partner_copy(index).wait()
         lane = lanes(block_n)
 
-        for source_slot in range(4):
-            zs, ys = source_slot // 2, source_slot % 2
+        def unpack_slot(source_slot, carry):
+            zs, ys = lax.div(source_slot, 2), lax.rem(source_slot, 2)
 
             def unpack(indices):
                 results = []
@@ -405,17 +430,19 @@
                     mine, theirs = gather_own[span, :], gather_other[span, :]
                     at_zero = jnp.where(xi == 0, mine, theirs)
                     at_one = jnp.where(xi == 0, theirs, mine)
-                    for group in range(4):
-                        half, colour = group // 2, group % 2
+                    for half in (0, 1):
                         plane = zs * (block_n // 2) + 2 * m + half
-                        left = turn(at_zero, plane - group * block_n)
-                        right = turn(at_one, plane + block_n - group * block_n)
-                        place = lax.rem(lane + LANES - plane, LANES)
-                        value = jnp.where(place < block_n, left, jnp.where(place < 2 * block_n, right, 0.0))
-                        results.append((colour, plane, value))
+                        place = lax.bitwise_and(lane + (LANES - plane), LANES - 1)
+                        low, middle = place < block_n, place < 2 * block_n
+                        for colour in (RED, BLACK):
+                            shift = plane - (2 * half + colour) * block_n
+                            right = lax.select(middle, turn(at_one, shift + block_n), jnp.zeros_like(at_one))
+                            results.append((colour, plane, lax.select(low, turn(at_zero, shift), right)))
                 for colour, plane, value in results:
                     coarse.g[colour][rows(plane * coarse.nb + ys * block_n, block_n), :] = value
             grouped(block_n // 4, GROUP, unpack)
+            return carry
+        lax.fori_loop(0, 4, unpack_slot, 0)
 
     def set_zero(ref, size):
         def step(i, carry):
@@ -530,7 +557,7 @@
                         results.append((colour, span, fine.v[colour][span, :] + change))
             for colour, span, value in results:
                 fine.v[colour][span, :] = value
-        grouped(fine.planes, 2, step)
+        grouped(fine.planes, 4, step)
 
     barrier = pltpu.get_barrier_semaphore()
     for target in ({'x': 1 - xi}, {'y': 1 - yi}, {'z': 1 - zi}, {'z': 1 - zi, 'y': 1 - yi}):
@@ -557,17 +584,19 @@
         load_copy(index, 0).wait()
         load_copy(index, 1).wait()
 
-        def step(i, inner):
-            k = index * (top.planes // load_chunks) + i
-            a, b = stage_u[rows(2 * k * edge, edge), :], stage_u[rows((2 * k + 1) * edge, edge), :]
-            top.v[RED][rows((k + 1) * top.pitch + TILE, edge), :] = turn(jnp.where(even_edge, a, b), skew(top, k))
-            top.v[BLACK][rows((k + 1) * top.pitch + TILE, edge), :] = turn(jnp.where(even_edge, b, a), skew(top, k))
-            a = stage_f[rows(2 * k * edge, edge), :] * scale
-            b = stage_f[rows((2 * k + 1) * edge, edge), :] * scale
-            top.g[RED][rows(k * edge, edge), :] = turn(jnp.where(even_edge, a, b), skew(top, k))
-            top.g[BLACK][rows(k * edge, edge), :] = turn(jnp.where(even_edge, b, a), skew(top, k))
-            return inner
-        return lax.fori_loop(0, top.planes // load_chunks, step, carry)
+        per_chunk = top.planes // load_chunks
+
+        def step(indices):
+            for i in indices:
+                k = index * per_chunk + i
+                for stage, target, start in ((stage_u, top.v, (k + 1) * top.pitch + TILE), (stage_f, top.g, k * edge)):
+                    a, b = stage[rows(2 * k * edge, edge), :], stage[rows((2 * k + 1) * edge, edge), :]
+                    if stage is stage_f:
+                        a, b = a * scale, b * scale
+                    target[RED][rows(start, edge), :] = turn(jnp.where(even_edge, a, b), skew(top, k))
+                    target[BLACK][rows(start, edge), :] = turn(jnp.where(even_edge, b, a), skew(top, k))
+        grouped(per_chunk, 2, step)
+        return carry
     lax.fori_loop(0, load_chunks, pack, 0)
 
     for index in range(len(levels) - 1):

time: 335 us -> 308 us (0.919)
  Pallas kernels: 335 us -> 308 us
    pallas_call x1, Pallas kernels: 325 us -> 298 us  [solve_packed(): pl.pallas_call(functools.partial(kernel_body, names, edge), out_shape=(ha...]
where the time goes in v3:
time: 308 us
  Pallas kernels  308 us (100%)
    pallas_call x1, Pallas kernels, solve_packed(): pl.pallas_call(functools.partial(kernel_body, names, edge), out_shape=(ha...  298 us
    pallas_call x1, Pallas kernels, unpack(): pl.pallas_call(unpack_body, grid=(edge // 2 // step,), out_shape=jax.Shap...  9.84 us

profile of v3, /device:TPU:0, one launch (start us, length us, event | category | flops | bytes accessed | tf_op | source)
XLA Modules:
  0.0 307.6 jit_solution(1451612577314411352)
XLA Ops:
  0.0 297.8 %multigrid.1 = (f32[8192,128]{1,0:T(8,128)}, f32[8192,128]{1,0:T(8,128)}) custom-call(f32[16384,128]{1,0:T(8,128)} %bitcast.4, f32[16384,128]{1,0:T(8,128)} %bitcast.5), custom_call_target="tpu_custom_call" | custom-call | tf_op jit(solution)/shard_map/multigrid/pallas_call | solution.py:737
  297.8 9.8 %unpack.1 = f32[128,128,128]{2,1,0:T(8,128)} custom-call(f32[64,128,128]{2,1,0:T(8,128)} %bitcast.6, f32[64,128,128]{2,1,0:T(8,128)} %bitcast.7), custom_call_target="tpu_custom_call" | custom-call | tf_op jit(solution)/shard_map/unpack/pallas_call | solution.py:762

commit v4 on v3

--- a/solution.py
+++ b/solution.py
@@ -637,10 +637,50 @@
             return carry
         lax.fori_loop(0, phases, phase, 0)
 
+    def solve_coarsest(level):
+        n, planes = level.n, level.planes
+        row = lax.broadcasted_iota(jnp.int32, (TILE, LANES), 0)
+        lane = lanes(TILE)
+        low_row, high_row = row == 0, row == n - 1
+        even_row = lax.rem(row, 2) == 0
+        odd_row = jnp.logical_not(even_row)
+
+        def spread(colour, k, x):
+            values = level.g[colour][rows(k * level.nb, TILE), :]
+            return jnp.broadcast_to(lax.slice(values, (0, x + k), (TILE, x + k + 1)), (TILE, LANES))
+        cells = [(k, x) for k in range(planes) for x in range(n)]
+        scaled = [{cell: spread(colour, *cell) for cell in cells} for colour in (RED, BLACK)]
+
+        def half(colour, own, other):
+            updated = {}
+            for k, x in cells:
+                minus, here = -own[k, x], other[k, x]
+                takes_below = even_row if (x + colour) % 2 == 0 else odd_row
+                total = lax.select(takes_below, other.get((k - 1, x), minus), other.get((k + 1, x), minus)) + here
+                total = total + (other.get((k, x - 1), minus) + other.get((k, x + 1), minus))
+                before = lax.select(low_row, minus, pltpu.roll(here, 1, 0))
+                total = total + (before + lax.select(high_row, minus, pltpu.roll(here, TILE - 1, 0)))
+                updated[k, x] = (total + scaled[colour][k, x]) * SIXTH
+            return updated
+
+        def sweep(index, state):
+            red, black = (dict(zip(cells, part)) for part in state)
+            red = half(RED, red, black)
+            black = half(BLACK, black, red)
+            return tuple(tuple(part[cell] for cell in cells) for part in (red, black))
+        zeros = (jnp.zeros((TILE, LANES), F32),) * len(cells)
+        state = lax.fori_loop(0, COARSE_SWEEPS, sweep, (zeros, zeros))
+        for colour, part in enumerate(state):
+            for k in range(planes):
+                plane = jnp.zeros((TILE, LANES), F32)
+                for x in range(n):
+                    plane = lax.select(lane == x + k, part[k * n + x], plane)
+                level.v[colour][rows((k + 1) * level.pitch + TILE, TILE), :] = plane
+
     def solve_local(index):
         level = levels[index]
         if index == len(levels) - 1:
-            solve(level, COARSE_SWEEPS, 1, None)
+            solve_coarsest(level)
             return
 
         def descend():
@@ -757,7 +797,7 @@
 
 
 def unpack(red, black, edge):
-    step = TILE
+    step = 2 * TILE
     spec = pl.BlockSpec((step, edge, LANES), lambda i: (i, 0, 0))
     return pl.pallas_call(
         unpack_body,

time: 308 us -> 300 us (0.974)
  Pallas kernels: 308 us -> 300 us
    pallas_call x1, Pallas kernels: 298 us -> 292 us  [solve_packed(): pl.pallas_call(functools.partial(kernel_body, names, edge), out_shape=(ha...]
where the time goes in v4:
time: 300 us
  Pallas kernels  300 us (100%)
    pallas_call x1, Pallas kernels, solve_packed(): pl.pallas_call(functools.partial(kernel_body, names, edge), out_shape=(ha...  292 us
    pallas_call x1, Pallas kernels, unpack(): pl.pallas_call(unpack_body, grid=(edge // 2 // step,), out_shape=jax.Shap...  7.88 us

profile of v4, /device:TPU:0, one launch (start us, length us, event | category | flops | bytes accessed | tf_op | source)
XLA Modules:
  0.0 299.6 jit_solution(17847942681708439765)
XLA Ops:
  0.0 291.7 %multigrid.1 = (f32[8192,128]{1,0:T(8,128)}, f32[8192,128]{1,0:T(8,128)}) custom-call(f32[16384,128]{1,0:T(8,128)} %bitcast.4, f32[16384,128]{1,0:T(8,128)} %bitcast.5), custom_call_target="tpu_custom_call" | custom-call | tf_op jit(solution)/shard_map/multigrid/pallas_call | solution.py:777
  291.7 7.9 %unpack.1 = f32[128,128,128]{2,1,0:T(8,128)} custom-call(f32[64,128,128]{2,1,0:T(8,128)} %bitcast.6, f32[64,128,128]{2,1,0:T(8,128)} %bitcast.7), custom_call_target="tpu_custom_call" | custom-call | tf_op jit(solution)/shard_map/unpack/pallas_call | solution.py:802
